TPU v7x, 512 devices: a whole 4x8x8 slice. The times are simulated.
512 devices in a mesh: gx: 4 (over y_hi), gy: 16 (over z, y_lo), gz: 8 (over x, core).
Axes of the slice: x: 4, y: 8 (y_hi: 4, y_lo: 2; y = y_hi * 2 + y_lo), z: 8, core: 2. Of those that a mesh axis runs over, the one named last changes fastest.
Arguments:
- nodal_scalar_values: float32 [3, 32, 128, 16384], P(None, 'gx', 'gy', 'gz'), may hold values from -6 to 6
- geometry: float32 [6, 4, 16, 2048], P(None, 'gx', 'gy', 'gz'), may hold values from -1.2 to 4, as said below
Outputs:
- assembled: float32 [3, 32, 128, 16384], P(None, 'gx', 'gy', 'gz')
Inputs may be any that keep to these rules, and one draw needn't show every extreme that they name: `geometry`: G00, G11 and G22 are positive; each off-diagonal factor is at most 0.3 times the root of the product of its two diagonal factors in magnitude.
All inputs are finite; a program needn't handle non-finite values.
Results may differ from a plain program's by a relative error of at most 0.00007.
Values sent between devices are 32-bit elements; how exact they have to be, the bound alone decides.
No kernel may reach another device: no remote copies, remote signals or barrier semaphores. Data moves between devices by JAX's collectives and lax.ppermute only.
A program may use at most 64 MiB of HBM per device.

v0:
```python
import math

import jax
import jax.numpy as jnp
import numpy as np
from jax import lax
from jax.sharding import PartitionSpec as P

interior_points = [
    -0.8717401485096066,
    -0.5917001814331423,
    -0.2092992179024789,
    0.2092992179024789,
    0.5917001814331423,
    0.8717401485096066,
]


def shifted(array, axis, by):
    count = lax.axis_size(axis)
    pairs = [(i, i + by) for i in range(count) if 0 <= i + by < count]
    return lax.ppermute(array, axis, pairs)


def legendre_seven(point):
    previous = 1.0
    current = point
    for order in range(1, 7):
        following = ((2 * order + 1) * point * current - order * previous) / (order + 1)
        previous = current
        current = following
    return current


def gll_tables():
    degree = 7
    points = [-1.0] + interior_points + [1.0]
    values = [legendre_seven(point) for point in points]
    node_count = degree + 1
    weights = np.array([2.0 / (degree * (degree + 1) * value * value) for value in values])
    derivative = np.zeros((node_count, node_count))
    for row_index in range(node_count):
        for col_index in range(node_count):
            if row_index != col_index:
                derivative[row_index, col_index] = values[row_index] / (
                    values[col_index] * (points[row_index] - points[col_index])
                )
    derivative[0, 0] = -degree * (degree + 1) / 4.0
    derivative[node_count - 1, node_count - 1] = degree * (degree + 1) / 4.0
    return (derivative, weights)


def apply_axis(field_in, matrix, direction):
    length = field_in.shape[direction]
    block_size = math.gcd(length, 128)
    big_table = jnp.kron(jnp.eye(block_size // 8, dtype=jnp.float32), matrix)
    dim_list = list(field_in.shape)
    folded_shape = (
        dim_list[:direction] + [length // block_size, block_size] + dim_list[direction + 1 :]
    )
    folded_field = field_in.reshape(folded_shape)
    patterns = ["nbyz,ab->nayz", "xnbz,ab->xnaz", "xynb,ab->xyna"]
    result = jnp.einsum(
        patterns[direction], folded_field, big_table, precision=lax.Precision.HIGHEST
    )
    return result.reshape(field_in.shape)


def expand(field_component, target):
    elem_x, elem_y, elem_z = field_component.shape
    spread = jnp.broadcast_to(
        field_component[:, None, :, None, :, None], (elem_x, 8, elem_y, 8, elem_z, 8)
    )
    return spread.reshape(target)


def stiffness(field_in, geometry):
    derivative, weights = gll_tables()
    matrix = jnp.asarray(derivative, jnp.float32)
    weight_row = jnp.asarray(weights, jnp.float32)
    size_x, size_y, size_z = field_in.shape
    weight_x = jnp.tile(weight_row, size_x // 8)
    weight_y = jnp.tile(weight_row, size_y // 8)
    weight_z = jnp.tile(weight_row, size_z // 8)
    node_weight = weight_x[:, None, None] * weight_y[None, :, None] * weight_z[None, None, :]
    grad_x = apply_axis(field_in, matrix, 0)
    grad_y = apply_axis(field_in, matrix, 1)
    grad_z = apply_axis(field_in, matrix, 2)
    factors = [expand(geometry[index], field_in.shape) for index in range(6)]
    flux_x = node_weight * (factors[0] * grad_x + factors[3] * grad_y + factors[4] * grad_z)
    flux_y = node_weight * (factors[3] * grad_x + factors[1] * grad_y + factors[5] * grad_z)
    flux_z = node_weight * (factors[4] * grad_x + factors[5] * grad_y + factors[2] * grad_z)
    transposed = matrix.T
    return (
        apply_axis(flux_x, transposed, 0)
        + apply_axis(flux_y, transposed, 1)
        + apply_axis(flux_z, transposed, 2)
    )


def combine(middle, below_plane, above_plane, direction):
    length = middle.shape[direction]
    from_above = jnp.concatenate(
        [lax.slice_in_dim(middle, 1, length, axis=direction), above_plane], axis=direction
    )
    from_below = jnp.concatenate(
        [below_plane, lax.slice_in_dim(middle, 0, length - 1, axis=direction)], axis=direction
    )
    position = lax.broadcasted_iota(jnp.int32, middle.shape, direction) % 8
    return (
        middle
        + jnp.where(position == 7, from_above, 0.0)
        + jnp.where(position == 0, from_below, 0.0)
    )


def edge_planes(summed, direction):
    length = summed.shape[direction]
    first_plane = lax.slice_in_dim(summed, 0, 1, axis=direction)
    last_plane = lax.slice_in_dim(summed, length - 1, length, axis=direction)
    return (first_plane, last_plane)


def local(nodal_scalar_values, geometry):
    component_count = nodal_scalar_values.shape[0]
    local_terms = jnp.stack(
        [
            stiffness(nodal_scalar_values[component], geometry)
            for component in range(component_count)
        ]
    )
    summed = local_terms
    first_plane, last_plane = edge_planes(summed, 1)
    below_plane = shifted(last_plane, "gx", 1)
    above_plane = shifted(first_plane, "gx", -1)
    summed = combine(summed, below_plane, above_plane, 1)
    first_plane, last_plane = edge_planes(summed, 2)
    below_plane = shifted(last_plane, "gy", 1)
    above_plane = shifted(first_plane, "gy", -1)
    summed = combine(summed, below_plane, above_plane, 2)
    first_plane, last_plane = edge_planes(summed, 3)
    below_plane = shifted(last_plane, "gz", 1)
    above_plane = shifted(first_plane, "gz", -1)
    summed = combine(summed, below_plane, above_plane, 3)
    return summed


def solution(mesh):
    return jax.shard_map(
        local,
        mesh=mesh,
        in_specs=(P(None, "gx", "gy", "gz"), P(None, "gx", "gy", "gz")),
        out_specs=P(None, "gx", "gy", "gz"),
        check_vma=False,
    )
```

profile of v0, /device:TPU:444, one launch (start us, length us, event | category | flops | bytes accessed | tf_op | source)
XLA Modules:
  0.0 80.4 jit_solution(14125740864815316012)
XLA Ops:
  0.0 1.6 %fusion.134 = (f32[1,8,8,2048]{3,2,1,0:T(8,128)S(1)}, f32[1,8,8,2048]{3,2,1,0:T(8,128)S(1)}, f32[1,8,8,2048]{3,2,1,0:T(8,128)S(1)}) fusion(f32[3,8,8,2048]{3,2,1,0:T(8,128)} %param.8), kind=kLoop, calls=%fused_computation.185 | loop fusion | bytes 3145728 | tf_op jit(solution)/shard_map/slice | solution.py:128
  3.6 0.8 fusion.32
  4.4 1.6 %copy_bitcast_fusion = (f32[8,8,16,128]{3,0,2,1:T(8,128)}, f32[8,8,16,128]{3,0,2,1:T(8,128)}) fusion(f32[1,8,8,2048]{3,2,1,0:T(8,128)S(1)} %get-tuple-element.19, f32[1,8,8,2048]{3,2,1,0:T(8,128)S(1)} %get-tuple-element.18), kind=kLoop, calls=%fused_computation.111 | loop fusion | bytes 2097152 | tf_op jit(solution)/shard_map/reshape;squeeze | solution.py:61
  6.1 0.8 fusion.42
  6.9 1.5 %broadcast_multiply_fusion = (f32[16,8,16,8]{3,2,1,0:T(8,128)}, f32[16,8,16,8]{3,2,1,0:T(8,128)}) fusion(f32[8,8]{1,0:T(8,128)S(1)} %copy-done.15, f32[16,16]{1,0:T(8,128)S(1)} %fusion.123, f32[8,8]{1,0:T(8,128)S(1)} %copy-done.16), kind=kLoop, calls=%fused_computation.107 | loop fusion | flops 32768 | bytes 132608 | tf_op jit(solution)/shard_map/jit(kron)/mul | solution.py:56
  8.4 1.6 %reshape.403 = f32[128,128,1,1]{1,0,2,3:T(8,128)S(1)} reshape(f32[16,8,16,8]{3,2,1,0:T(8,128)} %get-tuple-element.24) | data formatting | bytes 131072 | tf_op jit(solution)/shard_map/jit(kron)/mul | solution.py:56
  10.9 1.7 %reshape.406 = f32[128,128,1,1]{1,0,2,3:T(8,128)S(1)} reshape(f32[16,8,16,8]{3,2,1,0:T(8,128)} %get-tuple-element.23) | data formatting | bytes 131072 | tf_op jit(solution)/shard_map/jit(kron)/mul | solution.py:56
  12.9 2.4 %convolution_bitcast_fusion.3 = f32[8,8,16,128]{3,2,1,0:T(8,128)} fusion(f32[8,8,16,128]{3,0,2,1:T(8,128)} %get-tuple-element.32, f32[128,128,1,1]{1,0,2,3:T(8,128)S(1)} %reshape.403), kind=kOutput, calls=%fused_computation.40 | convolution fusion | flops 201326592 | bytes 1114112 | tf_op jit(solution)/shard_map/xynb,ab->xyna/dot_general | solution.py:63
  16.4 1.6 %convolution_bitcast_fusion.4 = f32[8,8,16,128]{3,2,1,0:T(8,128)S(1)} fusion(f32[8,8,16,128]{3,0,2,1:T(8,128)} %get-tuple-element.33, f32[128,128,1,1]{1,0,2,3:T(8,128)S(1)} %reshape.403), kind=kOutput, calls=%fused_computation.41 | convolution fusion | flops 201326592 | bytes 1114112 | tf_op jit(solution)/shard_map/xynb,ab->xyna/dot_general | solution.py:63
  18.0 3.2 %convolution_bitcast_fusion = f32[8,8,2048]{2,0,1:T(8,128)} fusion(f32[8,8,2048]{2,0,1:T(8,128)S(1)} %fusion.32, f32[8,8,16,128]{3,2,1,0:T(8,128)} %convolution_bitcast_fusion.3, f32[8,8,2048]{2,0,1:T(8,128)S(1)} %fusion.18, f32[2048]{0:T(1024)S(1)} %broadcast_in_dim.177, f32[2048]{0:T(1024)S(1)} %broadcast_in_dim.173, f32[2048]{0:T(1024)S(1)} %broadcast_in_dim.165, ...), kind=kOutput, calls=%fused_computation.18 | convolution fusion | flops 202244096 | bytes 2195712 | tf_op jit(solution)/shard_map/xynb,ab->xyna/dot_general | solution.py:63
  21.2 2.0 %convolution_bitcast_fusion.1 = f32[8,8,2048]{2,0,1:T(8,128)} fusion(f32[8,8,2048]{2,0,1:T(8,128)S(1)} %fusion.42, f32[8,8,16,128]{3,2,1,0:T(8,128)S(1)} %convolution_bitcast_fusion.4, f32[8,8,2048]{2,0,1:T(8,128)S(1)} %fusion.20, f32[2048]{0:T(1024)S(1)} %broadcast_in_dim.177, f32[2048]{0:T(1024)S(1)} %broadcast_in_dim.173, ...), kind=kOutput, calls=%fused_computation.19 | convolution fusion | flops 202244096 | bytes 2195712 | tf_op jit(solution)/shard_map/xynb,ab->xyna/dot_general | solution.py:63
  23.2 4.0 %multiply_multiply_fusion.7 = (f32[8,8,2048]{2,0,1:T(8,128)}, f32[8,8,2048]{2,0,1:T(8,128)}, f32[8,8,2048]{2,0,1:T(8,128)S(1)}, f32[8,8,2048]{2,0,1:T(8,128)}) fusion(f32[8,8,16,128]{3,2,1,0:T(8,128)S(1)} %convolution_bitcast_fusion.5, f32[8,8,2048]{2,0,1:T(8,128)S(1)} %fusion.22, f32[2048]{0:T(1024)S(1)} %broadcast_in_dim.173, ...), kind=kOutput, calls=%fused_computation.7 | convolution fusion | flops 15073280 | bytes 6849024 | tf_op jit(solution)/shard_map/nbyz,ab->nayz/dot_general | solution.py:63
  27.2 1.6 %fusion.54 = f32[8,8,2048]{2,0,1:T(8,128)} fusion(f32[8,8,1]{1,0,2:T(8,128)S(1)} %copy-done.12, f32[8,8,2048]{2,0,1:T(8,128)S(1)} %get-tuple-element.22), kind=kOutput, calls=%fused_computation.94 | convolution fusion | flops 12582912 | bytes 1048832 | tf_op jit(solution)/shard_map/xnbz,ab->xnaz/dot_general | solution.py:63
  29.0 1.9 %fusion.57 = f32[8,8,2048]{2,0,1:T(8,128)S(1)} fusion(f32[8,8,1]{1,0,2:T(8,128)S(1)} %copy-done.12, f32[8,8,2048]{2,0,1:T(8,128)} %get-tuple-element.21), kind=kOutput, calls=%fused_computation.97 | convolution fusion | flops 12582912 | bytes 1048832 | tf_op jit(solution)/shard_map/xnbz,ab->xnaz/dot_general | solution.py:63
  31.0 2.3 %convolution_bitcast_fusion.2 = f32[8,8,2048]{2,0,1:T(8,128)S(1)} fusion(f32[8,8,2048]{2,0,1:T(8,128)} %get-tuple-element.31, f32[8,8,16,128]{3,2,1,0:T(8,128)S(1)} %convolution_bitcast_fusion.5, f32[8,8,2048]{2,0,1:T(8,128)S(1)} %fusion.22, f32[2048]{0:T(1024)S(1)} %broadcast_in_dim.177, f32[2048]{0:T(1024)S(1)} %broadcast_in_dim.173, ...), kind=kOutput, calls=%fused_computation.20 | convolution fusion | flops 202244096 | bytes 2195712 | tf_op jit(solution)/shard_map/xynb,ab->xyna/dot_general | solution.py:63
  33.4 0.8 %fusion.60 = f32[8,8,2048]{2,0,1:T(8,128)S(1)} fusion(f32[8,8,1]{1,0,2:T(8,128)S(1)} %copy-done.12, f32[8,8,2048]{2,0,1:T(8,128)S(1)} %copy-done.11), kind=kOutput, calls=%fused_computation.100 | convolution fusion | flops 12582912 | bytes 1048832 | tf_op jit(solution)/shard_map/xnbz,ab->xnaz/dot_general | solution.py:63
  34.2 1.5 %fusion.5 = f32[1,8,8,2048]{3,1,2,0:T(8,128)S(1)} fusion(f32[8,8,2048]{2,0,1:T(8,128)S(1)} %copy-done.10, f32[8,8,1]{1,0,2:T(8,128)S(1)} %copy-done.12, f32[8,8,2048]{2,0,1:T(8,128)S(1)} %copy-done.8, f32[8,8,2048]{2,0,1:T(8,128)S(1)} %fusion.32, f32[8,8,16,128]{3,2,1,0:T(8,128)S(1)} %copy-done.1, f32[8,8,2048]{2,0,1:T(8,128)S(1)} %fusion.18, ...), kind=kOutput, calls=%fused_computation.17 | convolution fusion | flops 13762560 | bytes 3179008 | tf_op jit(solution)/shard_map/nbyz,ab->nayz/dot_general | solution.py:63
  35.7 1.4 %fusion.4 = f32[1,8,8,2048]{3,1,2,0:T(8,128)S(1)} fusion(f32[8,8,2048]{2,0,1:T(8,128)S(1)} %copy-done.9, f32[8,8,1]{1,0,2:T(8,128)S(1)} %copy-done.12, f32[8,8,2048]{2,0,1:T(8,128)S(1)} %fusion.57, f32[8,8,2048]{2,0,1:T(8,128)S(1)} %fusion.42, f32[8,8,16,128]{3,2,1,0:T(8,128)S(1)} %copy-done.3, f32[8,8,2048]{2,0,1:T(8,128)S(1)} %fusion.20, ...), kind=kOutput, calls=%fused_computation.16 | convolution fusion | flops 13762560 | bytes 3179008 | tf_op jit(solution)/shard_map/nbyz,ab->nayz/dot_general | solution.py:63
  37.2 1.4 %fusion.3 = f32[1,8,8,2048]{3,1,2,0:T(8,128)S(1)} fusion(f32[8,8,2048]{2,0,1:T(8,128)S(1)} %convolution_bitcast_fusion.2, f32[8,8,1]{1,0,2:T(8,128)S(1)} %copy-done.12, f32[8,8,2048]{2,0,1:T(8,128)S(1)} %fusion.60, f32[8,8,2048]{2,0,1:T(8,128)S(1)} %copy-done.5, f32[8,8,16,128]{3,2,1,0:T(8,128)S(1)} %convolution_bitcast_fusion.5, ...), kind=kOutput, calls=%fused_computation.15 | convolution fusion | flops 13762560 | bytes 3179008 | tf_op jit(solution)/shard_map/nbyz,ab->nayz/dot_general | solution.py:63
  39.0 4.0 %collective-permute-start = (f32[3,1,8,2048]{3,1,2,0:T(1,128)S(1)}, f32[3,1,8,2048]{3,1,2,0:T(1,128)S(1)}, u32[]{:S(2)}, u32[]{:S(2)}) collective-permute-start(f32[3,1,8,2048]{3,1,2,0:T(1,128)S(1)} %get-tuple-element.14), channel_id=1, source_target_pairs={{128,0},{256,128},{384,256},{129,1},{257,129},{385,257},{130,2},{2... | collective-permute-start | bytes 589832 | tf_op jit(solution)/shard_map/ppermute | solution.py:22
  43.1 1.3 %collective-permute-start.1 = (f32[3,1,8,2048]{3,1,2,0:T(1,128)S(1)}, f32[3,1,8,2048]{3,1,2,0:T(1,128)S(1)}, u32[]{:S(2)}, u32[]{:S(2)}) collective-permute-start(f32[3,1,8,2048]{3,1,2,0:T(1,128)S(1)} %get-tuple-element.13), channel_id=1, source_target_pairs={{0,128},{128,256},{256,384},{1,129},{129,257},{257,385},{2,130},{1... | collective-permute-start | bytes 589832 | tf_op jit(solution)/shard_map/ppermute | solution.py:22
  44.8 2.5 %collective-permute-done = f32[3,1,8,2048]{3,1,2,0:T(1,128)S(1)} collective-permute-done((f32[3,1,8,2048]{3,1,2,0:T(1,128)S(1)}, f32[3,1,8,2048]{3,1,2,0:T(1,128)S(1)}, u32[]{:S(2)}, u32[]{:S(2)}) %collective-permute-start) | collective-permute-done | bytes 196640 | tf_op jit(solution)/shard_map/ppermute | solution.py:22
  47.3 9.0 %collective-permute-done.1 = f32[3,1,8,2048]{3,1,2,0:T(1,128)S(1)} collective-permute-done((f32[3,1,8,2048]{3,1,2,0:T(1,128)S(1)}, f32[3,1,8,2048]{3,1,2,0:T(1,128)S(1)}, u32[]{:S(2)}, u32[]{:S(2)}) %collective-permute-start.1) | collective-permute-done | bytes 196640 | tf_op jit(solution)/shard_map/ppermute | solution.py:22
  56.2 0.8 fusion.7
  57.1 3.5 %collective-permute-start.2 = (f32[3,8,1,2048]{3,1,2,0:T(8,128)S(1)}, f32[3,8,1,2048]{3,1,2,0:T(8,128)S(1)}, u32[]{:S(2)}, u32[]{:S(2)}) collective-permute-start(f32[3,8,1,2048]{3,1,2,0:T(8,128)S(1)} %get-tuple-element.10), channel_id=1, source_target_pairs={{8,0},{16,8},{24,16},{32,24},{40,32},{48,40},{56,48},{64,56},{72,6... | collective-permute-start | bytes 589832 | tf_op jit(solution)/shard_map/ppermute | solution.py:22
  60.6 3.2 %collective-permute-start.3 = (f32[3,8,1,2048]{3,1,2,0:T(8,128)S(1)}, f32[3,8,1,2048]{3,1,2,0:T(8,128)S(1)}, u32[]{:S(2)}, u32[]{:S(2)}) collective-permute-start(f32[3,8,1,2048]{3,1,2,0:T(8,128)S(1)} %get-tuple-element.9), channel_id=1, source_target_pairs={{0,8},{8,16},{16,24},{24,32},{32,40},{40,48},{48,56},{56,64},{64,7... | collective-permute-start | bytes 589832 | tf_op jit(solution)/shard_map/ppermute | solution.py:22
  64.1 3.5 %collective-permute-done.2 = f32[3,8,1,2048]{3,1,2,0:T(8,128)S(1)} collective-permute-done((f32[3,8,1,2048]{3,1,2,0:T(8,128)S(1)}, f32[3,8,1,2048]{3,1,2,0:T(8,128)S(1)}, u32[]{:S(2)}, u32[]{:S(2)}) %collective-permute-start.2) | collective-permute-done | bytes 196640 | tf_op jit(solution)/shard_map/ppermute | solution.py:22
  67.6 1.6 %collective-permute-done.3 = f32[3,8,1,2048]{3,1,2,0:T(8,128)S(1)} collective-permute-done((f32[3,8,1,2048]{3,1,2,0:T(8,128)S(1)}, f32[3,8,1,2048]{3,1,2,0:T(8,128)S(1)}, u32[]{:S(2)}, u32[]{:S(2)}) %collective-permute-start.3) | collective-permute-done | bytes 196640 | tf_op jit(solution)/shard_map/ppermute | solution.py:22
  69.8 1.9 %collective-permute-start.4 = (f32[3,8,8,1]{3,1,2,0:T(8,128)S(1)}, f32[3,8,8,1]{3,1,2,0:T(8,128)S(1)}, u32[]{:S(2)}, u32[]{:S(2)}) collective-permute-start(f32[3,8,8,1]{3,1,2,0:T(8,128)S(1)} %get-tuple-element.6), channel_id=1, source_target_pairs={{1,0},{2,1},{3,2},{4,3},{5,4},{6,5},{7,6},{9,8},{10,9},{11,10},{12... | collective-permute-start | bytes 2312 | tf_op jit(solution)/shard_map/ppermute | solution.py:22
  71.7 2.4 %collective-permute-start.5 = (f32[3,8,8,1]{3,1,2,0:T(8,128)S(1)}, f32[3,8,8,1]{3,1,2,0:T(8,128)S(1)}, u32[]{:S(2)}, u32[]{:S(2)}) collective-permute-start(f32[3,8,8,1]{3,1,2,0:T(8,128)S(1)} %get-tuple-element.5), channel_id=1, source_target_pairs={{0,1},{1,2},{2,3},{3,4},{4,5},{5,6},{6,7},{8,9},{9,10},{10,11},{11... | collective-permute-start | bytes 2312 | tf_op jit(solution)/shard_map/ppermute | solution.py:22
  74.7 2.9 %collective-permute-done.5 = f32[3,8,8,1]{3,1,2,0:T(8,128)S(1)} collective-permute-done((f32[3,8,8,1]{3,1,2,0:T(8,128)S(1)}, f32[3,8,8,1]{3,1,2,0:T(8,128)S(1)}, u32[]{:S(2)}, u32[]{:S(2)}) %collective-permute-start.5) | collective-permute-done | bytes 800 | tf_op jit(solution)/shard_map/ppermute | solution.py:22
  78.3 2.1 %copy.76 = f32[3,8,8,2048]{3,2,1,0:T(8,128)} copy(f32[3,8,8,2048]{3,1,2,0:T(8,128)S(1)} %fusion.11) | data formatting | bytes 3145728 | tf_op jit(solution)/shard_map/add | solution.py:111
  (70 shorter events, 7.3 us)
Async XLA Ops:
  0.0 1.9 %copy-start.4 = (f32[3,8,8,2048]{3,2,1,0:T(8,128)S(1)}, f32[3,8,8,2048]{3,2,1,0:T(8,128)}, u32[]{:S(2)}) copy-start(f32[3,8,8,2048]{3,2,1,0:T(8,128)} %param.8) | copy-start | bytes 4718596
  0.0 1.9 %copy-start.12 = (f32[8,8,1]{1,0,2:T(8,128)S(1)}, f32[8,8,1]{1,0,2:T(8,128)}, u32[]{:S(2)}) copy-start(f32[8,8,1]{1,0,2:T(8,128)} %constant.40) | copy-start | bytes 772
  1.9 10.7 %copy-start.6 = (f32[1,8,8,2048]{3,2,1,0:T(8,128)}, f32[1,8,8,2048]{3,2,1,0:T(8,128)S(1)}, u32[]{:S(2)}) copy-start(f32[1,8,8,2048]{3,2,1,0:T(8,128)S(1)} %get-tuple-element.17) | copy-start | bytes 1572868
  4.4 2.5 %copy-start.15 = (f32[8,8]{1,0:T(8,128)S(1)}, f32[8,8]{1,0:T(8,128)}, u32[]{:S(2)}) copy-start(f32[8,8]{1,0:T(8,128)} %constant.39) | copy-start | bytes 772
  4.4 2.4 %copy-start.16 = (f32[8,8]{1,0:T(8,128)S(1)}, f32[8,8]{1,0:T(8,128)}, u32[]{:S(2)}) copy-start(f32[8,8]{1,0:T(8,128)} %constant.35.clone) | copy-start | bytes 772
  6.9 3.2 %copy-start.13 = (f32[6,1,1,256]{3,2,1,0:T(1,128)S(1)}, f32[6,1,1,256]{3,2,1,0:T(1,128)}, u32[]{:S(2)}) copy-start(f32[6,1,1,256]{3,2,1,0:T(1,128)} %param.9) | copy-start | bytes 18436
  6.9 3.8 %copy-start.14 = (f32[8]{0:T(128)S(1)}, f32[8]{0:T(128)}, u32[]{:S(2)}) copy-start(f32[8]{0:T(128)} %constant.36.clone) | copy-start | bytes 100
  18.0 5.2 %copy-start.2 = (f32[8,8,16,128]{3,2,1,0:T(8,128)}, f32[8,8,16,128]{3,2,1,0:T(8,128)S(1)}, u32[]{:S(2)}) copy-start(f32[8,8,16,128]{3,2,1,0:T(8,128)S(1)} %convolution_bitcast_fusion.4) | copy-start | bytes 1572868
  21.2 2.0 %copy-start = (f32[8,8,16,128]{3,2,1,0:T(8,128)S(1)}, f32[8,8,16,128]{3,2,1,0:T(8,128)}, u32[]{:S(2)}) copy-start(f32[8,8,16,128]{3,2,1,0:T(8,128)} %convolution_bitcast_fusion.3) | copy-start | bytes 1572868
  21.2 2.0 %copy-start.7 = (f32[1,8,8,2048]{3,2,1,0:T(8,128)S(1)}, f32[1,8,8,2048]{3,2,1,0:T(8,128)}, u32[]{:S(2)}) copy-start(f32[1,8,8,2048]{3,2,1,0:T(8,128)} %copy-done.6) | copy-start | bytes 1572868
  29.0 4.3 %copy-start.11 = (f32[8,8,2048]{2,0,1:T(8,128)S(1)}, f32[8,8,2048]{2,0,1:T(8,128)}, u32[]{:S(2)}) copy-start(f32[8,8,2048]{2,0,1:T(8,128)} %get-tuple-element.20) | copy-start | bytes 1572868
  31.0 3.2 %copy-start.1 = (f32[8,8,16,128]{3,2,1,0:T(8,128)S(1)}, f32[8,8,16,128]{3,2,1,0:T(8,128)}, u32[]{:S(2)}) copy-start(f32[8,8,16,128]{3,2,1,0:T(8,128)} %convolution_bitcast_fusion.3) | copy-start | bytes 1572868
  31.0 3.2 %copy-start.8 = (f32[8,8,2048]{2,0,1:T(8,128)S(1)}, f32[8,8,2048]{2,0,1:T(8,128)}, u32[]{:S(2)}) copy-start(f32[8,8,2048]{2,0,1:T(8,128)} %fusion.54) | copy-start | bytes 1572868
  31.0 3.2 %copy-start.10 = (f32[8,8,2048]{2,0,1:T(8,128)S(1)}, f32[8,8,2048]{2,0,1:T(8,128)}, u32[]{:S(2)}) copy-start(f32[8,8,2048]{2,0,1:T(8,128)} %convolution_bitcast_fusion) | copy-start | bytes 1572868
  34.2 1.5 %copy-start.3 = (f32[8,8,16,128]{3,2,1,0:T(8,128)S(1)}, f32[8,8,16,128]{3,2,1,0:T(8,128)}, u32[]{:S(2)}) copy-start(f32[8,8,16,128]{3,2,1,0:T(8,128)} %copy-done.2) | copy-start | bytes 1572868
  34.2 1.5 %copy-start.9 = (f32[8,8,2048]{2,0,1:T(8,128)S(1)}, f32[8,8,2048]{2,0,1:T(8,128)}, u32[]{:S(2)}) copy-start(f32[8,8,2048]{2,0,1:T(8,128)} %convolution_bitcast_fusion.1) | copy-start | bytes 1572868
  35.7 1.5 %copy-start.5 = (f32[8,8,2048]{2,0,1:T(8,128)S(1)}, f32[8,8,2048]{2,0,1:T(8,128)}, u32[]{:S(2)}) copy-start(f32[8,8,2048]{2,0,1:T(8,128)} %get-tuple-element.31) | copy-start | bytes 1572868
  39.0 8.2 %collective-permute-start = (f32[3,1,8,2048]{3,1,2,0:T(1,128)S(1)}, f32[3,1,8,2048]{3,1,2,0:T(1,128)S(1)}, u32[]{:S(2)}, u32[]{:S(2)}) collective-permute-start(f32[3,1,8,2048]{3,1,2,0:T(1,128)S(1)} %get-tuple-element.14), channel_id=1, source_target_pairs={{128,0},{256,128},{384,256},{129,1},{257,129},{385,257},{130,2},{2... | collective-permute-start | bytes 589832 | tf_op jit(solution)/shard_map/ppermute | solution.py:22
  43.1 13.1 %collective-permute-start.1 = (f32[3,1,8,2048]{3,1,2,0:T(1,128)S(1)}, f32[3,1,8,2048]{3,1,2,0:T(1,128)S(1)}, u32[]{:S(2)}, u32[]{:S(2)}) collective-permute-start(f32[3,1,8,2048]{3,1,2,0:T(1,128)S(1)} %get-tuple-element.13), channel_id=1, source_target_pairs={{0,128},{128,256},{256,384},{1,129},{129,257},{257,385},{2,130},{1... | collective-permute-start | bytes 589832 | tf_op jit(solution)/shard_map/ppermute | solution.py:22
  57.1 10.6 %collective-permute-start.2 = (f32[3,8,1,2048]{3,1,2,0:T(8,128)S(1)}, f32[3,8,1,2048]{3,1,2,0:T(8,128)S(1)}, u32[]{:S(2)}, u32[]{:S(2)}) collective-permute-start(f32[3,8,1,2048]{3,1,2,0:T(8,128)S(1)} %get-tuple-element.10), channel_id=1, source_target_pairs={{8,0},{16,8},{24,16},{32,24},{40,32},{48,40},{56,48},{64,56},{72,6... | collective-permute-start | bytes 589832 | tf_op jit(solution)/shard_map/ppermute | solution.py:22
  60.6 8.6 %collective-permute-start.3 = (f32[3,8,1,2048]{3,1,2,0:T(8,128)S(1)}, f32[3,8,1,2048]{3,1,2,0:T(8,128)S(1)}, u32[]{:S(2)}, u32[]{:S(2)}) collective-permute-start(f32[3,8,1,2048]{3,1,2,0:T(8,128)S(1)} %get-tuple-element.9), channel_id=1, source_target_pairs={{0,8},{8,16},{16,24},{24,32},{32,40},{40,48},{48,56},{56,64},{64,7... | collective-permute-start | bytes 589832 | tf_op jit(solution)/shard_map/ppermute | solution.py:22
  69.8 4.9 %collective-permute-start.4 = (f32[3,8,8,1]{3,1,2,0:T(8,128)S(1)}, f32[3,8,8,1]{3,1,2,0:T(8,128)S(1)}, u32[]{:S(2)}, u32[]{:S(2)}) collective-permute-start(f32[3,8,8,1]{3,1,2,0:T(8,128)S(1)} %get-tuple-element.6), channel_id=1, source_target_pairs={{1,0},{2,1},{3,2},{4,3},{5,4},{6,5},{7,6},{9,8},{10,9},{11,10},{12... | collective-permute-start | bytes 2312 | tf_op jit(solution)/shard_map/ppermute | solution.py:22
  71.7 5.9 %collective-permute-start.5 = (f32[3,8,8,1]{3,1,2,0:T(8,128)S(1)}, f32[3,8,8,1]{3,1,2,0:T(8,128)S(1)}, u32[]{:S(2)}, u32[]{:S(2)}) collective-permute-start(f32[3,8,8,1]{3,1,2,0:T(8,128)S(1)} %get-tuple-element.5), channel_id=1, source_target_pairs={{0,1},{1,2},{2,3},{3,4},{4,5},{5,6},{6,7},{8,9},{9,10},{10,11},{11... | collective-permute-start | bytes 2312 | tf_op jit(solution)/shard_map/ppermute | solution.py:22
where the time goes:
time: 80.9 us; the launch traced here: 80.4 us
  matrix products  28.2 us (35%)
  waiting for transfers between devices  19.4 us (24%)
  starting transfers between devices  16.4 us (20%)
  local copies, waits for them, and re-layouts  12.2 us (15%)
  other arithmetic  3.76 us (5%)
    dot_general x18, matrix products, apply_axis(): jnp.einsum(patterns[direction], folded_field, big_table, precision=lax.Pr...  28.2 us
    ppermute x6, waiting for transfers between devices, shifted(): return lax.ppermute(array, axis, pairs)  19.4 us
    ppermute x6, starting transfers between devices, shifted(): return lax.ppermute(array, axis, pairs)  16.4 us
    mul x2, local copies, waits for them, and re-layouts, apply_axis(): big_table = jnp.kron(jnp.eye(block_size // 8, dtype=jnp.float32), matrix)  3.3 us
    add x1, local copies, waits for them, and re-layouts, combine(): middle + jnp.where(position == 7, from_above, 0.0)  2.06 us
    add x3, other arithmetic, combine(): middle + jnp.where(position == 7, from_above, 0.0)  2 us
  transfers between devices with their start and end apart: 6, of which 5 were waited for; matrix products, arithmetic and copies ran while one was open for 2% of the time, Pallas kernels for 0%

commit v1 on v0

v1 whole, which is shorter than its diff:
```python
import functools

import jax
import jax.numpy as jnp
import numpy as np
from jax import lax
from jax.experimental import pallas as pl
from jax.experimental.pallas import tpu as pltpu
from jax.sharding import PartitionSpec as P

interior_points = [
    -0.8717401485096066,
    -0.5917001814331423,
    -0.2092992179024789,
    0.2092992179024789,
    0.5917001814331423,
    0.8717401485096066,
]
LANES = 128
BLOCK = 256
F32 = jnp.float32
BF16 = jnp.bfloat16


def legendre_seven(point):
    previous = 1.0
    current = point
    for order in range(1, 7):
        following = ((2 * order + 1) * point * current - order * previous) / (order + 1)
        previous = current
        current = following
    return current


def gll_tables():
    degree = 7
    points = [-1.0] + interior_points + [1.0]
    values = [legendre_seven(point) for point in points]
    node_count = degree + 1
    weights = np.array([2.0 / (degree * (degree + 1) * value * value) for value in values])
    derivative = np.zeros((node_count, node_count))
    for row_index in range(node_count):
        for col_index in range(node_count):
            if row_index != col_index:
                derivative[row_index, col_index] = values[row_index] / (
                    values[col_index] * (points[row_index] - points[col_index])
                )
    derivative[0, 0] = -degree * (degree + 1) / 4.0
    derivative[node_count - 1, node_count - 1] = degree * (degree + 1) / 4.0
    return (derivative.astype(np.float32).astype(np.float64), weights)


def split_table(table):
    high = np.asarray(table, np.float32).astype(jnp.bfloat16)
    low = (np.asarray(table, np.float64) - high.astype(np.float64)).astype(jnp.bfloat16)
    return high, low


def tables():
    derivative, weights = gll_tables()
    eye = np.eye(8)
    grads = np.concatenate([np.kron(derivative, eye), np.kron(eye, derivative)], 0)
    high, low = split_table(grads)
    grad_xy = np.concatenate([high, high, low], 1)
    plane = np.kron(weights, weights)
    back_x = np.kron((derivative * weights[:, None]).T, np.diag(weights))
    back_y = np.kron(np.diag(weights), (derivative * weights[:, None]).T)
    high, low = split_table(np.concatenate([back_x, back_y], 1))
    back_xy = np.concatenate([high, high, low], 1)
    many = np.eye(BLOCK // 8)
    grad_z = np.concatenate(split_table(np.kron(many, derivative.T)), 0)
    back_z = np.concatenate(split_table(np.kron(many, derivative)), 0)
    spread = np.kron(np.eye(LANES)[:, : BLOCK // 8], np.ones((1, 8))).astype(jnp.bfloat16)
    weight_z = np.tile(weights, BLOCK // 8)[None].astype(np.float32)
    plane = np.tile(plane[:, None], (1, BLOCK)).astype(np.float32)
    return grad_xy, back_xy, grad_z, back_z, spread, weight_z, plane


def split(values):
    high = values.astype(BF16)
    return high, (values - high.astype(F32)).astype(BF16)


def dot(left, right):
    return jnp.dot(left, right, preferred_element_type=F32)


def lane_iota():
    return lax.broadcasted_iota(jnp.int32, (8, LANES), 1)


def stiffness_kernel(
    u_ref, geo_ref, gxy_ref, bxy_ref, gz_ref, bz_ref, spread_ref, wz_ref, plane_ref,
    out_ref, xa_ref, xb_ref, yf_ref, za_ref, zb_ref, geo_scr,
):
    components = u_ref.shape[0]
    length = u_ref.shape[3]
    blocks = length // BLOCK
    tiles = length // LANES
    per_block = BLOCK // 8
    geo = jnp.concatenate([geo_ref[...], jnp.zeros((2, geo_ref.shape[1]), F32)], 0)
    rows = []
    for block in range(blocks):
        start = block * per_block
        tile = geo[:, start // LANES * LANES : start // LANES * LANES + LANES]
        shift = start % LANES
        rows.append(pltpu.roll(tile, LANES - shift, 1) if shift else tile)
    stacked = jnp.concatenate(rows, 0)
    first, rest = split(stacked)
    rest = stacked - first.astype(F32)
    second = rest.astype(BF16)
    third = (rest - second.astype(F32)).astype(BF16)
    spread = spread_ref[...]
    expanded = dot(first, spread) + dot(second, spread) + dot(third, spread)
    geo_scr[...] = expanded * wz_ref[...]

    def body(block, carry):
        start = pl.multiple_of(block * BLOCK, BLOCK)
        where = pl.ds(start, BLOCK)
        field = jnp.concatenate(
            [u_ref[c, :, :, where].reshape(64, BLOCK) for c in range(components)], 0
        )
        high, low = split(field)
        grad_z = (
            dot(high, gz_ref[:BLOCK]) + dot(low, gz_ref[:BLOCK]) + dot(high, gz_ref[BLOCK:])
        )
        factor = geo_scr[pl.ds(pl.multiple_of(block * 8, 8), 8), :]
        g = [factor[k : k + 1] for k in range(6)]
        fluxes = []
        sums = []
        for c in range(components):
            mine = slice(64 * c, 64 * c + 64)
            stack = jnp.concatenate([high[mine], low[mine], high[mine]], 0)
            both = dot(gxy_ref[...], stack)
            gx, gy, gz = both[:64], both[64:], grad_z[mine]
            fx = g[0] * gx + g[3] * gy + g[4] * gz
            fy = g[3] * gx + g[1] * gy + g[5] * gz
            fz = g[4] * gx + g[5] * gy + g[2] * gz
            fluxes.append(fz * plane_ref[...])
            fh, fl = split(jnp.concatenate([fx, fy], 0))
            sums.append(dot(bxy_ref[...], jnp.concatenate([fh, fl, fh], 0)))
        fh, fl = split(jnp.concatenate(fluxes, 0))
        back = dot(fh, bz_ref[:BLOCK]) + dot(fl, bz_ref[:BLOCK]) + dot(fh, bz_ref[BLOCK:])
        for c in range(components):
            total = sums[c] + back[64 * c : 64 * c + 64]
            out_ref[c, :, :, where] = total.reshape(8, 8, BLOCK)
        return carry

    lax.fori_loop(0, blocks, body, 0)

    position = lax.broadcasted_iota(jnp.int32, (8, length), 1)
    last = (position % 8 == 7) & (position != length - 1)
    initial = (position % 8 == 0) & (position != 0)
    for c in range(components):
        for x in range(8):
            row = out_ref[c, x]
            after = pltpu.roll(row, length - 1, 1)
            before = pltpu.roll(row, 1, 1)
            out_ref[c, x] = (
                row + jnp.where(last, after, 0.0) + jnp.where(initial, before, 0.0)
            )

    even_x = lax.rem(lax.axis_index("gx"), 2) == 0
    even_z = lax.rem(lax.axis_index("gz"), 2) == 0
    for c in range(components):
        for t in range(tiles):
            where = slice(t * LANES, t * LANES + LANES)
            first_plane = out_ref[c, 0, :, where]
            last_plane = out_ref[c, 7, :, where]
            xa_ref[c * tiles + t] = jnp.where(even_x, last_plane, first_plane)
            xb_ref[c * tiles + t] = jnp.where(even_x, first_plane, last_plane)
        for y, k in ((0, 0), (7, 1)):
            for x in range(8):
                yf_ref[k, c, x : x + 1, :] = out_ref[c, x, y : y + 1, :]
    lane = lane_iota()
    low_plane = jnp.zeros((8, LANES), F32)
    high_plane = jnp.zeros((8, LANES), F32)
    for c in range(components):
        for x in range(8):
            slot = 8 * c + x
            begin = out_ref[c, x, :, :LANES]
            end = out_ref[c, x, :, length - LANES :]
            begin = pltpu.roll(begin, slot, 1) if slot else begin
            end = pltpu.roll(end, slot + 1, 1)
            low_plane = jnp.where(lane == slot, begin, low_plane)
            high_plane = jnp.where(lane == slot, end, high_plane)
    za_ref[...] = jnp.where(even_z, high_plane, low_plane)
    zb_ref[...] = jnp.where(even_z, low_plane, high_plane)


def z_halo(za_ref, zb_ref):
    even_z = lax.rem(lax.axis_index("gz"), 2) == 0
    first, second = za_ref[...], zb_ref[...]
    return jnp.where(even_z, second, first), jnp.where(even_z, first, second)


def at_lane(packed, slot, lane_to):
    lane = lane_iota()
    shift = (lane_to - slot) % LANES
    moved = pltpu.roll(packed, shift, 1) if shift else packed
    return jnp.where(lane == lane_to, moved, 0.0)


def x_face_kernel(xa_ref, xb_ref, za_ref, zb_ref, outa_ref, outb_ref):
    tiles = 16
    components = xa_ref.shape[0] // tiles
    even_x = lax.rem(lax.axis_index("gx"), 2) == 0
    low, high = z_halo(za_ref, zb_ref)
    outa_ref[...] = xa_ref[...]
    outb_ref[...] = xb_ref[...]
    for c in range(components):
        for t, packed, lane_to in ((0, low, 0), (tiles - 1, high, LANES - 1)):
            first = at_lane(packed, 8 * c, lane_to)
            last = at_lane(packed, 8 * c + 7, lane_to)
            spot = c * tiles + t
            outa_ref[spot] = xa_ref[spot] + jnp.where(even_x, last, first)
            outb_ref[spot] = xb_ref[spot] + jnp.where(even_x, first, last)


def y_face_kernel(yf_ref, xa_ref, xb_ref, za_ref, zb_ref, outa_ref, outb_ref):
    tiles = 16
    components = yf_ref.shape[1]
    even_x = lax.rem(lax.axis_index("gx"), 2) == 0
    even_y = lax.rem(lax.axis_index("gy"), 2) == 0
    low, high = z_halo(za_ref, zb_ref)
    sublane = lax.broadcasted_iota(jnp.int32, (8, LANES), 0)
    lane = lane_iota()
    for c in range(components):
        halos = {}
        for t, packed, lane_to in ((0, low, 0), (tiles - 1, high, LANES - 1)):
            pieces = [jnp.zeros((8, LANES), F32)] * 2
            for k, y in ((0, 0), (1, 7)):
                for x in range(8):
                    slot = 8 * c + x
                    shift = (lane_to - slot) % LANES
                    moved = pltpu.roll(packed, shift, 1) if shift else packed
                    moved = jnp.broadcast_to(moved[y : y + 1], (8, LANES))
                    pieces[k] = jnp.where((lane == lane_to) & (sublane == x), moved, pieces[k])
            halos[t] = pieces
        for t in range(tiles):
            spot = c * tiles + t
            where = slice(t * LANES, t * LANES + LANES)
            ra, rb = xa_ref[spot], xb_ref[spot]
            below = jnp.where(even_x, rb, ra)
            above = jnp.where(even_x, ra, rb)
            sides = []
            for k, y in ((0, 0), (1, 7)):
                value = yf_ref[k, c, :, where]
                value = value + jnp.where(sublane == 0, jnp.broadcast_to(below[y : y + 1], (8, LANES)), 0.0)
                value = value + jnp.where(sublane == 7, jnp.broadcast_to(above[y : y + 1], (8, LANES)), 0.0)
                if t in halos:
                    value = value + halos[t][k]
                sides.append(value)
            outa_ref[spot] = jnp.where(even_y, sides[1], sides[0])
            outb_ref[spot] = jnp.where(even_y, sides[0], sides[1])


def final_kernel(local_ref, xa_ref, xb_ref, ya_ref, yb_ref, za_ref, zb_ref, out_ref):
    tiles = 16
    components = local_ref.shape[0]
    even_x = lax.rem(lax.axis_index("gx"), 2) == 0
    even_y = lax.rem(lax.axis_index("gy"), 2) == 0
    low, high = z_halo(za_ref, zb_ref)
    sublane = lax.broadcasted_iota(jnp.int32, (8, LANES), 0)
    for c in range(components):
        for t in range(tiles):
            spot = c * tiles + t
            where = slice(t * LANES, t * LANES + LANES)
            ra, rb = xa_ref[spot], xb_ref[spot]
            below = jnp.where(even_x, rb, ra)
            above = jnp.where(even_x, ra, rb)
            ya, yb = ya_ref[spot], yb_ref[spot]
            front = jnp.where(even_y, yb, ya)
            behind = jnp.where(even_y, ya, yb)
            for x in range(8):
                value = local_ref[c, x, :, where]
                if x == 0:
                    value = value + below
                if x == 7:
                    value = value + above
                value = value + jnp.where(
                    sublane == 0, jnp.broadcast_to(front[x : x + 1], (8, LANES)), 0.0
                )
                value = value + jnp.where(
                    sublane == 7, jnp.broadcast_to(behind[x : x + 1], (8, LANES)), 0.0
                )
                if t == 0:
                    value = value + at_lane(low, 8 * c + x, 0)
                if t == tiles - 1:
                    value = value + at_lane(high, 8 * c + x, LANES - 1)
                out_ref[c, x, :, where] = value


def pair_exchange(first, second, axis):
    count = lax.axis_size(axis)

    def pairs(start):
        found = []
        for i in range(start, count - 1, 2):
            found += [(i, i + 1), (i + 1, i)]
        return found

    return lax.ppermute(first, axis, pairs(0)), lax.ppermute(second, axis, pairs(1))


def call(kernel, outs, scratch=(), flops=1000000):
    return pl.pallas_call(
        kernel,
        out_shape=[jax.ShapeDtypeStruct(shape, F32) for shape in outs],
        scratch_shapes=list(scratch),
        compiler_params=pltpu.CompilerParams(vmem_limit_bytes=24 * 1024 * 1024),
        cost_estimate=pl.CostEstimate(flops=flops, bytes_accessed=1000000, transcendentals=0),
    )


def local(nodal, geometry):
    components, _, _, length = nodal.shape
    tiles = length // LANES
    geo = geometry.reshape(6, length // 8)
    face = (components * tiles, 8, LANES)
    tile = (8, LANES)
    result, xa, xb, yf, za, zb = call(
        stiffness_kernel,
        [nodal.shape, face, face, (2, components, 8, length), tile, tile],
        [pltpu.VMEM((8 * length // BLOCK, BLOCK), F32)],
    )(nodal, geo, *[jnp.asarray(table) for table in tables()])
    za, zb = pair_exchange(za, zb, "gz")
    xa, xb = call(x_face_kernel, [face, face])(xa, xb, za, zb)
    xa, xb = pair_exchange(xa, xb, "gx")
    ya, yb = call(y_face_kernel, [face, face])(yf, xa, xb, za, zb)
    ya, yb = pair_exchange(ya, yb, "gy")
    (result,) = call(final_kernel, [nodal.shape])(result, xa, xb, ya, yb, za, zb)
    return result


def solution(mesh):
    return jax.shard_map(
        local,
        mesh=mesh,
        in_specs=(P(None, "gx", "gy", "gz"), P(None, "gx", "gy", "gz")),
        out_specs=P(None, "gx", "gy", "gz"),
        check_vma=False,
    )
```

time: 80.9 us -> 56.7 us (0.70)
  the two profiles are of different devices: /device:TPU:444 before, /device:TPU:236 now
where the time goes in v1:
time: 56.7 us; the launch traced here: 56.1 us
  starting transfers between devices  21.6 us (38%)
  waiting for transfers between devices  18.1 us (32%)
  Pallas kernels  8.25 us (15%)
  local copies, waits for them, and re-layouts  7.99 us (14%)
    ppermute x3, starting transfers between devices, pair_exchange(): lax.ppermute(first, axis, pairs(0))  11.4 us
    ppermute x3, waiting for transfers between devices, pair_exchange(): lax.ppermute(second, axis, pairs(1))  11 us
    ppermute x3, starting transfers between devices, pair_exchange(): lax.ppermute(second, axis, pairs(1))  10.2 us
    unnamed x17, local copies, waits for them, and re-layouts  7.99 us
    ppermute x3, waiting for transfers between devices, pair_exchange(): lax.ppermute(first, axis, pairs(0))  7.09 us
    pallas_call x1, Pallas kernels, local(): call(stiffness_kernel, [nodal.shape, face, face, (2, components, 8, lengt...  6.47 us
    pallas_call x1, Pallas kernels, local(): result, = call(final_kernel, [nodal.shape])(result, xa, xb, ya, yb, za, zb)  1.53 us
  transfers between devices with their start and end apart: 6, of which 5 were waited for; matrix products, arithmetic and copies ran while one was open for 0% of the time, Pallas kernels for 0%

profile of v1, /device:TPU:236, one launch (start us, length us, event | category | flops | bytes accessed | tf_op | source)
XLA Modules:
  0.0 56.1 jit_solution(7239322414702829866)
XLA Ops:
  0.0 0.7 %copy.12 = f32[6,1,1,256]{3,0,1,2:T(8,128)S(1)} copy(f32[6,1,1,256]{3,2,1,0:T(1,128)} %param.10) | data formatting | bytes 12288
  0.7 0.0 copy-start
  0.7 1.4 %copy-done = f32[3,8,8,2048]{3,2,1,0:T(8,128)S(1)} copy-done((f32[3,8,8,2048]{3,2,1,0:T(8,128)S(1)}, f32[3,8,8,2048]{3,2,1,0:T(8,128)}, u32[]{:S(2)}) %copy-start) | copy-done | bytes 1572888
  2.1 0.0 copy-start.1
  2.1 0.9 %copy-done.1 = bf16[512,256]{1,0:T(8,128)(2,1)S(1)} copy-done((bf16[512,256]{1,0:T(8,128)(2,1)S(1)}, bf16[512,256]{1,0:T(8,128)(2,1)}, u32[]{:S(2)}) %copy-start.1) | copy-done | bytes 262168
  3.1 0.0 copy-start.2
  3.1 0.9 %copy-done.2 = bf16[512,256]{1,0:T(8,128)(2,1)S(1)} copy-done((bf16[512,256]{1,0:T(8,128)(2,1)S(1)}, bf16[512,256]{1,0:T(8,128)(2,1)}, u32[]{:S(2)}) %copy-start.2) | copy-done | bytes 262168
  4.0 0.0 copy-start.3
  4.0 0.8 %copy-done.3 = f32[64,256]{1,0:T(8,128)S(1)} copy-done((f32[64,256]{1,0:T(8,128)S(1)}, f32[64,256]{1,0:T(8,128)}, u32[]{:S(2)}) %copy-start.3) | copy-done | bytes 65560
  4.8 0.0 copy-start.4
  4.8 0.8 %copy-done.4 = bf16[128,256]{1,0:T(8,128)(2,1)S(1)} copy-done((bf16[128,256]{1,0:T(8,128)(2,1)S(1)}, bf16[128,256]{1,0:T(8,128)(2,1)}, u32[]{:S(2)}) %copy-start.4) | copy-done | bytes 65560
  5.7 0.0 copy-start.5
  5.7 0.8 %copy-done.5 = bf16[128,192]{1,0:T(8,128)(2,1)S(1)} copy-done((bf16[128,192]{1,0:T(8,128)(2,1)S(1)}, bf16[128,192]{1,0:T(8,128)(2,1)}, u32[]{:S(2)}) %copy-start.5) | copy-done | bytes 49176
  6.5 0.0 copy-start.6
  6.5 0.8 %copy-done.6 = bf16[64,384]{1,0:T(8,128)(2,1)S(1)} copy-done((bf16[64,384]{1,0:T(8,128)(2,1)S(1)}, bf16[64,384]{1,0:T(8,128)(2,1)}, u32[]{:S(2)}) %copy-start.6) | copy-done | bytes 49176
  7.3 0.7 %copy-done.7 = f32[1,256]{1,0:T(1,128)S(1)} copy-done((f32[1,256]{1,0:T(1,128)S(1)}, f32[1,256]{1,0:T(1,128)}, u32[]{:S(2)}) %copy-start.7) | copy-done | bytes 1048
  8.0 6.5 %shard_map.91 = (f32[3,8,8,2048]{3,2,1,0:T(8,128)S(1)}, f32[48,8,128]{2,1,0:T(8,128)S(1)}, f32[48,8,128]{2,1,0:T(8,128)S(1)}, f32[2,3,8,2048]{3,2,1,0:T(8,128)S(...) custom-call(f32[3,8,8,2048]{3,2,1,0:T(8,128)S(1)} %copy-done, f32[6,256]{1,0:T(8,128)S(1)} %bitcast.3, ...), custom_call_target="tpu_custom_call" | custom-call | flops 1000000 | bytes 1000000 | tf_op jit(solution)/shard_map/pallas_call | solution.py:322
  14.5 1.9 %collective-permute-start = (f32[8,128]{1,0:T(8,128)S(1)}, f32[8,128]{1,0:T(8,128)S(1)}, u32[]{:S(2)}, u32[]{:S(2)}) collective-permute-start(f32[8,128]{1,0:T(8,128)S(1)} %get-tuple-element.18), channel_id=1, source_target_pairs={{0,1},{1,0},{2,3},{3,2},{4,5},{5,4},{6,7},{7,6},{8,9},{9,8},{10,11... | collective-permute-start | bytes 12296 | tf_op jit(solution)/shard_map/ppermute | solution.py:303
  16.4 2.6 %collective-permute-start.1 = (f32[8,128]{1,0:T(8,128)S(1)}, f32[8,128]{1,0:T(8,128)S(1)}, u32[]{:S(2)}, u32[]{:S(2)}) collective-permute-start(f32[8,128]{1,0:T(8,128)S(1)} %get-tuple-element.19), channel_id=1, source_target_pairs={{1,2},{2,1},{3,4},{4,3},{5,6},{6,5},{9,10},{10,9},{11,12},{12,11},... | collective-permute-start | bytes 12296 | tf_op jit(solution)/shard_map/ppermute | solution.py:303
  19.0 0.0 collective-permute-done.za_ref
  19.0 2.4 %collective-permute-done.1.zb_ref = f32[8,128]{1,0:T(8,128)S(1)} collective-permute-done((f32[8,128]{1,0:T(8,128)S(1)}, f32[8,128]{1,0:T(8,128)S(1)}, u32[]{:S(2)}, u32[]{:S(2)}) %collective-permute-start.1) | collective-permute-done | bytes 4128 | tf_op jit(solution)/shard_map/ppermute | solution.py:303
  21.3 0.1 shard_map.92
  21.4 2.7 %collective-permute-start.2 = (f32[48,8,128]{2,1,0:T(8,128)S(1)}, f32[48,8,128]{2,1,0:T(8,128)S(1)}, u32[]{:S(2)}, u32[]{:S(2)}) collective-permute-start(f32[48,8,128]{2,1,0:T(8,128)S(1)} %get-tuple-element.20), channel_id=1, source_target_pairs={{0,128},{128,0},{256,384},{384,256},{1,129},{129,1},{257,385},{385... | collective-permute-start | bytes 589832 | tf_op jit(solution)/shard_map/ppermute | solution.py:303
  24.1 2.7 %collective-permute-start.3 = (f32[48,8,128]{2,1,0:T(8,128)S(1)}, f32[48,8,128]{2,1,0:T(8,128)S(1)}, u32[]{:S(2)}, u32[]{:S(2)}) collective-permute-start(f32[48,8,128]{2,1,0:T(8,128)S(1)} %get-tuple-element.21), channel_id=1, source_target_pairs={{128,256},{256,128},{129,257},{257,129},{130,258},{258,130},{131,2... | collective-permute-start | bytes 589832 | tf_op jit(solution)/shard_map/ppermute | solution.py:303
  26.8 6.3 %collective-permute-done.2.xa_ref = f32[48,8,128]{2,1,0:T(8,128)S(1)} collective-permute-done((f32[48,8,128]{2,1,0:T(8,128)S(1)}, f32[48,8,128]{2,1,0:T(8,128)S(1)}, u32[]{:S(2)}, u32[]{:S(2)}) %collective-permute-start.2) | collective-permute-done | bytes 196640 | tf_op jit(solution)/shard_map/ppermute | solution.py:303
  33.1 2.6 %collective-permute-done.3.xb_ref = f32[48,8,128]{2,1,0:T(8,128)S(1)} collective-permute-done((f32[48,8,128]{2,1,0:T(8,128)S(1)}, f32[48,8,128]{2,1,0:T(8,128)S(1)}, u32[]{:S(2)}, u32[]{:S(2)}) %collective-permute-start.3) | collective-permute-done | bytes 196640 | tf_op jit(solution)/shard_map/ppermute | solution.py:303
  35.7 0.2 shard_map.93
  35.9 6.8 %collective-permute-start.4 = (f32[48,8,128]{2,1,0:T(8,128)S(1)}, f32[48,8,128]{2,1,0:T(8,128)S(1)}, u32[]{:S(2)}, u32[]{:S(2)}) collective-permute-start(f32[48,8,128]{2,1,0:T(8,128)S(1)} %get-tuple-element.23), channel_id=1, source_target_pairs={{0,8},{8,0},{16,24},{24,16},{32,40},{40,32},{48,56},{56,48},{64,72... | collective-permute-start | bytes 589832 | tf_op jit(solution)/shard_map/ppermute | solution.py:303
  42.7 5.0 %collective-permute-start.5 = (f32[48,8,128]{2,1,0:T(8,128)S(1)}, f32[48,8,128]{2,1,0:T(8,128)S(1)}, u32[]{:S(2)}, u32[]{:S(2)}) collective-permute-start(f32[48,8,128]{2,1,0:T(8,128)S(1)} %get-tuple-element.24), channel_id=1, source_target_pairs={{8,16},{16,8},{24,32},{32,24},{40,48},{48,40},{56,64},{64,56},{72,... | collective-permute-start | bytes 589832 | tf_op jit(solution)/shard_map/ppermute | solution.py:303
  47.7 0.8 %collective-permute-done.4.ya_ref = f32[48,8,128]{2,1,0:T(8,128)S(1)} collective-permute-done((f32[48,8,128]{2,1,0:T(8,128)S(1)}, f32[48,8,128]{2,1,0:T(8,128)S(1)}, u32[]{:S(2)}, u32[]{:S(2)}) %collective-permute-start.4) | collective-permute-done | bytes 196640 | tf_op jit(solution)/shard_map/ppermute | solution.py:303
  48.4 6.1 %collective-permute-done.5.yb_ref = f32[48,8,128]{2,1,0:T(8,128)S(1)} collective-permute-done((f32[48,8,128]{2,1,0:T(8,128)S(1)}, f32[48,8,128]{2,1,0:T(8,128)S(1)}, u32[]{:S(2)}, u32[]{:S(2)}) %collective-permute-start.5) | collective-permute-done | bytes 196640 | tf_op jit(solution)/shard_map/ppermute | solution.py:303
  54.6 1.5 %shard_map.94 = f32[3,8,8,2048]{3,2,1,0:T(8,128)} custom-call(f32[3,8,8,2048]{3,2,1,0:T(8,128)S(1)} %get-tuple-element.15.local_ref, f32[48,8,128]{2,1,0:T(8,128)S(1)} %collective-permute-done.2.xa_ref, f32[48,8,128]{2,1,0:T(8,128)S(1)} %collective-permute-done.3.xb_ref, f32[48,8,128]{2,1,0:T(8,128)S(1)} %collective-permute-done.4.ya_ref, ...), custom_call_target="tpu_custom_call" | custom-call | flops 1000000 | bytes 1000000 | tf_op jit(solution)/shard_map/pallas_call | solution.py:332
  (1 shorter events, 0.0 us)
Async XLA Ops:
  0.7 1.4 %copy-start = (f32[3,8,8,2048]{3,2,1,0:T(8,128)S(1)}, f32[3,8,8,2048]{3,2,1,0:T(8,128)}, u32[]{:S(2)}) copy-start(f32[3,8,8,2048]{3,2,1,0:T(8,128)} %u_ref.1) | copy-start | bytes 4718596
  2.1 0.9 %copy-start.1 = (bf16[512,256]{1,0:T(8,128)(2,1)S(1)}, bf16[512,256]{1,0:T(8,128)(2,1)}, u32[]{:S(2)}) copy-start(bf16[512,256]{1,0:T(8,128)(2,1)} %constant.17.clone.bz_ref) | copy-start | bytes 786436
  3.1 0.9 %copy-start.2 = (bf16[512,256]{1,0:T(8,128)(2,1)S(1)}, bf16[512,256]{1,0:T(8,128)(2,1)}, u32[]{:S(2)}) copy-start(bf16[512,256]{1,0:T(8,128)(2,1)} %constant.16.clone.gz_ref) | copy-start | bytes 786436
  4.0 0.8 %copy-start.3 = (f32[64,256]{1,0:T(8,128)S(1)}, f32[64,256]{1,0:T(8,128)}, u32[]{:S(2)}) copy-start(f32[64,256]{1,0:T(8,128)} %constant.20.clone.plane_ref) | copy-start | bytes 196612
  4.8 0.8 %copy-start.4 = (bf16[128,256]{1,0:T(8,128)(2,1)S(1)}, bf16[128,256]{1,0:T(8,128)(2,1)}, u32[]{:S(2)}) copy-start(bf16[128,256]{1,0:T(8,128)(2,1)} %constant.18.clone.spread_ref) | copy-start | bytes 196612
  5.7 0.8 %copy-start.5 = (bf16[128,192]{1,0:T(8,128)(2,1)S(1)}, bf16[128,192]{1,0:T(8,128)(2,1)}, u32[]{:S(2)}) copy-start(bf16[128,192]{1,0:T(8,128)(2,1)} %constant.14.clone.gxy_ref) | copy-start | bytes 147460
  6.5 0.8 %copy-start.6 = (bf16[64,384]{1,0:T(8,128)(2,1)S(1)}, bf16[64,384]{1,0:T(8,128)(2,1)}, u32[]{:S(2)}) copy-start(bf16[64,384]{1,0:T(8,128)(2,1)} %constant.15.clone.bxy_ref) | copy-start | bytes 147460
  7.3 0.7 %copy-start.7 = (f32[1,256]{1,0:T(1,128)S(1)}, f32[1,256]{1,0:T(1,128)}, u32[]{:S(2)}) copy-start(f32[1,256]{1,0:T(1,128)} %constant.19.clone.wz_ref) | copy-start | bytes 3076
  14.5 4.5 %collective-permute-start = (f32[8,128]{1,0:T(8,128)S(1)}, f32[8,128]{1,0:T(8,128)S(1)}, u32[]{:S(2)}, u32[]{:S(2)}) collective-permute-start(f32[8,128]{1,0:T(8,128)S(1)} %get-tuple-element.18), channel_id=1, source_target_pairs={{0,1},{1,0},{2,3},{3,2},{4,5},{5,4},{6,7},{7,6},{8,9},{9,8},{10,11... | collective-permute-start | bytes 12296 | tf_op jit(solution)/shard_map/ppermute | solution.py:303
  16.4 4.9 %collective-permute-start.1 = (f32[8,128]{1,0:T(8,128)S(1)}, f32[8,128]{1,0:T(8,128)S(1)}, u32[]{:S(2)}, u32[]{:S(2)}) collective-permute-start(f32[8,128]{1,0:T(8,128)S(1)} %get-tuple-element.19), channel_id=1, source_target_pairs={{1,2},{2,1},{3,4},{4,3},{5,6},{6,5},{9,10},{10,9},{11,12},{12,11},... | collective-permute-start | bytes 12296 | tf_op jit(solution)/shard_map/ppermute | solution.py:303
  21.4 11.7 %collective-permute-start.2 = (f32[48,8,128]{2,1,0:T(8,128)S(1)}, f32[48,8,128]{2,1,0:T(8,128)S(1)}, u32[]{:S(2)}, u32[]{:S(2)}) collective-permute-start(f32[48,8,128]{2,1,0:T(8,128)S(1)} %get-tuple-element.20), channel_id=1, source_target_pairs={{0,128},{128,0},{256,384},{384,256},{1,129},{129,1},{257,385},{385... | collective-permute-start | bytes 589832 | tf_op jit(solution)/shard_map/ppermute | solution.py:303
  24.1 11.6 %collective-permute-start.3 = (f32[48,8,128]{2,1,0:T(8,128)S(1)}, f32[48,8,128]{2,1,0:T(8,128)S(1)}, u32[]{:S(2)}, u32[]{:S(2)}) collective-permute-start(f32[48,8,128]{2,1,0:T(8,128)S(1)} %get-tuple-element.21), channel_id=1, source_target_pairs={{128,256},{256,128},{129,257},{257,129},{130,258},{258,130},{131,2... | collective-permute-start | bytes 589832 | tf_op jit(solution)/shard_map/ppermute | solution.py:303
  35.9 12.6 %collective-permute-start.4 = (f32[48,8,128]{2,1,0:T(8,128)S(1)}, f32[48,8,128]{2,1,0:T(8,128)S(1)}, u32[]{:S(2)}, u32[]{:S(2)}) collective-permute-start(f32[48,8,128]{2,1,0:T(8,128)S(1)} %get-tuple-element.23), channel_id=1, source_target_pairs={{0,8},{8,0},{16,24},{24,16},{32,40},{40,32},{48,56},{56,48},{64,72... | collective-permute-start | bytes 589832 | tf_op jit(solution)/shard_map/ppermute | solution.py:303
  42.7 11.9 %collective-permute-start.5 = (f32[48,8,128]{2,1,0:T(8,128)S(1)}, f32[48,8,128]{2,1,0:T(8,128)S(1)}, u32[]{:S(2)}, u32[]{:S(2)}) collective-permute-start(f32[48,8,128]{2,1,0:T(8,128)S(1)} %get-tuple-element.24), channel_id=1, source_target_pairs={{8,16},{16,8},{24,32},{32,24},{40,48},{48,40},{56,64},{64,56},{72,... | collective-permute-start | bytes 589832 | tf_op jit(solution)/shard_map/ppermute | solution.py:303
